TPU v7x, 32 devices: a whole 2x2x4 slice. The times are simulated.
32 devices in a mesh: ga: 2 (over core), band: 16 (over z, y, x).
Axes of the slice: x: 2, y: 2, z: 4, core: 2. Of those that a mesh axis runs over, the one named last changes fastest.
Arguments:
- orbitals: bfloat16 [1024, 2, 16384], P('band', None, 'ga'), may hold values from -6 to 6
- projectors: bfloat16 [864, 2, 16384], P(None, None, ('ga', 'band')), may hold values from -0.03125 to 0.03125
- coupling: float32 [4, 18, 18], replicated, may hold values from -6 to 6
- species: int32 [48], replicated, may hold values from 0 to 3
- offsets: int32 [48], replicated, may hold values from 0 to 846, as said below
Outputs:
- applied: bfloat16 [1024, 2, 16384], P('band', None, 'ga')
Inputs may be any that keep to these rules, and one draw needn't show every extreme that they name: Each atom's 18 projectors are the 18 consecutive rows of projectors starting at its offset; offsets are multiples of 18, and the atoms' blocks are distinct and cover all 864 rows.
All inputs are finite; a program needn't handle non-finite values.
Results may differ from a plain program's by a relative error of at most 0.0049.
Values may be sent and summed in bfloat16 or wider, within the bound.
A program may use at most 64 MiB of HBM per device.

v0:
```python
import jax
import jax.numpy as jnp
from jax import lax
from jax.sharding import PartitionSpec as P


def block_matrices(coupling, species, offsets):
    per_atom = coupling.shape[1]
    count = offsets.shape[0]
    blocks = jnp.arange(count, dtype=jnp.int32)
    matches = (offsets[None, :] == blocks[:, None] * per_atom).astype(jnp.int32)
    atom_kind = jnp.sum(matches * species[None, :], axis=1)
    onehot = (atom_kind[:, None] == jnp.arange(coupling.shape[0], dtype=jnp.int32)[None, :]).astype(
        jnp.float32
    )
    table = coupling.reshape(coupling.shape[0], per_atom * per_atom)
    picked = jnp.dot(
        onehot, table, precision=lax.Precision.HIGHEST, preferred_element_type=jnp.float32
    )
    return picked.reshape(count, per_atom, per_atom)


def apply_coupling(matrices, becp):
    count = matrices.shape[0]
    per_atom = matrices.shape[1]
    height = becp.shape[0]
    widths = becp.shape[2]
    blocked = becp.reshape(count, per_atom, 2 * widths)
    coupled = jnp.einsum("aij,ajc->aic", matrices, blocked, precision=lax.Precision.HIGHEST)
    return coupled.reshape(height, 2, widths).astype(jnp.bfloat16)


def project_bands(projectors, spread):
    total_proj = projectors.shape[0]
    total_bands = spread.shape[0]
    flat_proj = projectors.reshape(total_proj, -1)
    turned = jnp.concatenate([spread[:, 1, :], -spread[:, 0, :]], axis=1)
    stacked = jnp.concatenate([spread.reshape(total_bands, -1), turned], axis=0)
    partial_value = lax.dot_general(
        flat_proj, stacked, (((1,), (1,)), ((), ())), preferred_element_type=jnp.float32
    )
    return partial_value.reshape(total_proj, 2, total_bands)


def add_back(projectors, dbecp):
    total_proj = projectors.shape[0]
    total_bands = dbecp.shape[2]
    columns = dbecp.reshape(total_proj, 2 * total_bands)
    real_part = lax.dot_general(
        columns, projectors[:, 0, :], (((0,), (0,)), ((), ())), preferred_element_type=jnp.float32
    )
    imag_part = lax.dot_general(
        columns, projectors[:, 1, :], (((0,), (0,)), ((), ())), preferred_element_type=jnp.float32
    )
    out_real = real_part[:total_bands] - imag_part[total_bands:]
    out_imag = imag_part[:total_bands] + real_part[total_bands:]
    return jnp.stack([out_real, out_imag], axis=1).astype(jnp.bfloat16)


def per_device(orbitals, projectors, coupling, species, offsets):
    matrices = block_matrices(coupling, species, offsets)
    spread = lax.all_to_all(orbitals, "band", split_axis=2, concat_axis=0, tiled=True)
    partial_value = project_bands(projectors, spread)
    becp = lax.psum(partial_value, ("ga", "band"))
    dbecp = apply_coupling(matrices, becp)
    result = add_back(projectors, dbecp)
    return lax.all_to_all(result, "band", split_axis=0, concat_axis=2, tiled=True)


def solution(mesh):
    placed = (P("band", None, "ga"), P(None, None, ("ga", "band")), P(), P(), P())
    return jax.shard_map(
        per_device, mesh=mesh, in_specs=placed, out_specs=P("band", None, "ga"), check_vma=False
    )
```

profile of v0, /device:TPU:0, one launch (start us, length us, event | category | flops | bytes accessed | tf_op | source)
XLA Modules:
  0.0 417.0 jit_solution(8911082358564989493)
XLA Ops:
  6.5 11.4 %copy.45 = bf16[64,2,8192]{0,1,2:T(2,128)(2,1)} copy(bf16[64,2,8192]{2,1,0:T(2,128)(2,1)} %param.5) | data formatting | bytes 4194304 | tf_op args[0]
  17.9 7.5 %reshape.39 = bf16[16,2,32768]{2,1,0:T(2,128)(2,1)} reshape(bf16[8192,2,64]{2,1,0:T(2,128)(2,1)} %bitcast.46) | data formatting | bytes 4194304
  25.4 8.5 %all-to-all-start = ((bf16[16,2,32768]{2,1,0:T(2,128)(2,1)}), bf16[16,2,32768]{2,1,0:T(2,128)(2,1)}, u32[]{:S(2)}, u32[]{:S(2)}) async-start(bf16[16,2,32768]{2,1,0:T(2,128)(2,1)} %reshape.39), calls=%async_computation | async-start | bytes 4194304 | tf_op jit(solution)/shard_map/all_to_all | solution.py:62
  34.0 0.5 copy.60
  34.5 42.6 %all-to-all-done = bf16[16,2,32768]{2,1,0:T(2,128)(2,1)} async-done(((bf16[16,2,32768]{2,1,0:T(2,128)(2,1)}), bf16[16,2,32768]{2,1,0:T(2,128)(2,1)}, u32[]{:S(2)}, u32[]{:S(2)}) %all-to-all-start) | async-done | bytes 2097184 | tf_op jit(solution)/shard_map/all_to_all | solution.py:62
  77.1 7.4 %reshape.40 = bf16[8192,2,64]{2,1,0:T(2,128)(2,1)} reshape(bf16[16,2,32768]{2,1,0:T(2,128)(2,1)} %all-to-all-done) | data formatting | bytes 4194304
  84.4 10.6 %copy.55 = bf16[64,2,16,512]{3,0,2,1:T(8,128)(2,1)} copy(bf16[64,2,16,512]{0,1,3,2:T(2,128)(2,1)} %bitcast.44) | data formatting | bytes 4194304 | tf_op jit(solution)/shard_map/all_to_all | solution.py:62
  95.0 7.4 %copy.54 = bf16[64,2,16,512]{3,2,0,1:T(8,128)(2,1)} copy(bf16[64,2,16,512]{0,1,3,2:T(2,128)(2,1)} %bitcast.45) | data formatting | bytes 4194304 | tf_op jit(solution)/shard_map/all_to_all | solution.py:62
  102.4 1.8 slice_bitcast_fusion
  104.6 2.2 copy.47
  106.8 0.6 copy.59
  107.4 12.5 %fusion.6 = f32[864,2048]{1,0:T(8,128)} fusion(bf16[864,1024]{1,0:T(8,128)(2,1)S(1)} %bitcast.53, bf16[1024,512]{1,0:T(8,128)(2,1)S(1)} %get-tuple-element.8, bf16[1024,512]{1,0:T(8,128)(2,1)S(1)} %get-tuple-element.7, bf16[1024,1024]{1,0:T(8,128)(2,1)S(1)} %bitcast.52), kind=kOutput, calls=%fused_computation.6 | convolution fusion | flops 3636461568 | bytes 13041664 | tf_op jit(solution)/shard_map/dot_general | solution.py:39
  119.9 7.9 %reshape.36 = f32[48,18,2048]{2,1,0:T(8,128)} reshape(f32[864,2048]{1,0:T(8,128)} %fusion.6) | data formatting | bytes 14155776 | tf_op jit(solution)/shard_map/reshape | solution.py:28
  127.8 0.7 copy-done.5
  129.7 4.2 %fusion.22 = (bf16[864,1,512]{2,1,0:T(2,128)(2,1)}, bf16[864,1,512]{2,1,0:T(2,128)(2,1)}) fusion(bf16[864,2,512]{2,1,0:T(2,128)(2,1)S(1)} %copy-done), kind=kLoop, calls=%fused_computation.30 | loop fusion | bytes 3538944 | tf_op jit(solution)/shard_map/slice | solution.py:53
  133.9 189.5 %all-reduce.2.cloned.1.call-done = f32[48,18,2048]{2,1,0:T(8,128)} async-done(((f32[48,18,2048]{2,1,0:T(8,128)}), f32[48,18,2048]{2,1,0:T(8,128)}) %all-reduce.2.cloned.1.call-update) | async-done | bytes 7077904 | tf_op jit(solution)/shard_map/psum | solution.py:64
  323.4 12.2 %convolution_convert_fusion = bf16[48,18,2048]{2,1,0:T(8,128)(2,1)} fusion(f32[48,18,18]{2,1,0:T(8,128)S(1)} %copy.49, f32[48,18,2048]{2,1,0:T(8,128)} %all-reduce.2.cloned.1.call-done), kind=kOutput, calls=%fused_computation.7 | convolution fusion | flops 383975424 | bytes 10679040 | tf_op jit(solution)/shard_map/aij,ajc->aic/dot_general | solution.py:29
  335.5 6.2 %convert_element_type.12 = bf16[864,2048]{1,0:T(8,128)(2,1)} reshape(bf16[48,18,2048]{2,1,0:T(8,128)(2,1)} %convolution_convert_fusion) | data formatting | bytes 7077888 | tf_op jit(solution)/shard_map/convert_element_type | solution.py:30
  341.8 4.6 %fusion.14 = f32[2048,512]{1,0:T(8,128)S(1)} fusion(bf16[864,2048]{1,0:T(8,128)(2,1)} %convert_element_type.12, bf16[864,1,512]{2,1,0:T(2,128)(2,1)S(1)} %copy-done.4), kind=kOutput, calls=%fused_computation.19 | convolution fusion | flops 1811939328 | bytes 8617984 | tf_op jit(solution)/shard_map/dot_general | solution.py:52
  346.4 2.4 fusion.15
  348.8 1.2 fusion.11
  350.2 2.2 copy.52
  352.4 54.2 %all_to_all.36 = bf16[1024,2,512]{2,1,0:T(2,128)(2,1)S(1)} all-to-all(bf16[1024,2,512]{2,1,0:T(2,128)(2,1)S(1)} %copy.52), channel_id=1, replica_groups=mesh['ga'=2,'band'=16] {'band'}, dimensions={0} | all-to-all | bytes 4194304 | tf_op jit(solution)/shard_map/all_to_all | solution.py:67
  406.5 3.6 copy.58
  (25 shorter events, 1.7 us)
Async XLA Ops:
  25.4 8.6 %copy-start = (bf16[864,2,512]{2,1,0:T(2,128)(2,1)S(1)}, bf16[864,2,512]{2,1,0:T(2,128)(2,1)}, u32[]{:S(2)}) copy-start(bf16[864,2,512]{2,1,0:T(2,128)(2,1)} %param.6) | copy-start | bytes 5308420
  25.4 51.6 %all-to-all-start = ((bf16[16,2,32768]{2,1,0:T(2,128)(2,1)}), bf16[16,2,32768]{2,1,0:T(2,128)(2,1)}, u32[]{:S(2)}, u32[]{:S(2)}) async-start(bf16[16,2,32768]{2,1,0:T(2,128)(2,1)} %reshape.39), calls=%async_computation | async-start | bytes 4194304 | tf_op jit(solution)/shard_map/all_to_all | solution.py:62
  34.0 289.4 %all-reduce.2.cloned.1.call-start = ((), (), s32[]{:S(2)}) async-start(), calls=%async_computation.2 | async-start | bytes 18874368 | tf_op jit(solution)/shard_map/psum | solution.py:64
  102.4 2.2 copy-start.1
  127.8 0.8 copy-start.5
  127.8 1.0 copy-start.6
  127.8 1.0 copy-start.7
  335.5 6.2 %copy-start.4 = (bf16[864,1,512]{2,1,0:T(2,128)(2,1)S(1)}, bf16[864,1,512]{2,1,0:T(2,128)(2,1)}, u32[]{:S(2)}) copy-start(bf16[864,1,512]{2,1,0:T(2,128)(2,1)} %get-tuple-element.9) | copy-start | bytes 2654212
  341.7 4.6 %copy-start.2 = (bf16[864,2048]{1,0:T(8,128)(2,1)S(1)}, bf16[864,2048]{1,0:T(8,128)(2,1)}, u32[]{:S(2)}) copy-start(bf16[864,2048]{1,0:T(8,128)(2,1)} %convert_element_type.12) | copy-start | bytes 10616836
  341.7 4.6 %copy-start.3 = (bf16[864,1,512]{2,1,0:T(2,128)(2,1)S(1)}, bf16[864,1,512]{2,1,0:T(2,128)(2,1)}, u32[]{:S(2)}) copy-start(bf16[864,1,512]{2,1,0:T(2,128)(2,1)} %get-tuple-element.10) | copy-start | bytes 2654212
Sparse Core Ops, SparseCore 0:
  127.9 195.3 all-reduce.1
where the time goes:
time: 419 us; the launch traced here: 417 us
  waiting for transfers between devices  232 us (55%)
  local copies, waits for them, and re-layouts  73.2 us (17%)
  blocking collectives  54.2 us (13%)
  matrix products  32 us (8%)
  between operations  13.6 us (3%)
  starting transfers between devices  8.57 us (2%)
    psum x1, waiting for transfers between devices, per_device(): becp = lax.psum(partial_value, ('ga', 'band'))  189 us
    all_to_all x1, blocking collectives, per_device(): lax.all_to_all(result, 'band', split_axis=0, concat_axis=2, tiled=True)  54.2 us
    all_to_all x1, waiting for transfers between devices, per_device(): lax.all_to_all(orbitals, 'band', split_axis=2, concat_axis=0, tiled=True)  42.6 us
    unnamed x22, local copies, waits for them, and re-layouts  28.5 us
    all_to_all x3, local copies, waits for them, and re-layouts, per_device(): lax.all_to_all(orbitals, 'band', split_axis=2, concat_axis=0, tiled=True)  20.1 us
    dot_general x1, matrix products, project_bands(): lax.dot_general(flat_proj, stacked, (((1,), (1,)), ((), ())), preferred_e...  12.5 us
    dot_general x1, matrix products, apply_coupling(): jnp.einsum('aij,ajc->aic', matrices, blocked, precision=lax.Precision.HIG...  12.2 us
    all_to_all x1, starting transfers between devices, per_device(): lax.all_to_all(orbitals, 'band', split_axis=2, concat_axis=0, tiled=True)  8.52 us
  transfers between devices with their start and end apart: 2, of which 2 were waited for; matrix products, arithmetic and copies ran while one was open for 1% of the time, Pallas kernels for 0%

commit v1 on v0

--- a/solution.py
+++ b/solution.py
@@ -59,7 +59,10 @@
 
 def per_device(orbitals, projectors, coupling, species, offsets):
     matrices = block_matrices(coupling, species, offsets)
-    spread = lax.all_to_all(orbitals, "band", split_axis=2, concat_axis=0, tiled=True)
+    spread = jnp.concatenate(
+        lax.all_to_all(jnp.stack(jnp.split(orbitals, lax.axis_size("band"), axis=2)), "band", 0, 0),
+        axis=0,
+    )
     partial_value = project_bands(projectors, spread)
     becp = lax.psum(partial_value, ("ga", "band"))
     dbecp = apply_coupling(matrices, becp)

time: 419 us -> 394 us (0.940)
  local copies, waits for them, and re-layouts: 73.2 us -> 55 us
    all_to_all x3 -> x1, local copies, waits for them, and re-layouts: 20.1 us -> 0.45 us  [per_device(): lax.all_to_all(jnp.stack(jnp.split(orbitals, lax.axis_size('band'), axis=...]
    unnamed x22 -> x30, local copies, waits for them, and re-layouts: 28.5 us -> 30.1 us
  transfers between devices with their start and end apart: 2 -> 2, of which waited for: 2 -> 2; matrix products, arithmetic and copies ran while one was open for 1% -> 2% of each run, Pallas kernels for 0% -> 0%
where the time goes in v1:
time: 394 us
  waiting for transfers between devices  229 us (58%)
  local copies, waits for them, and re-layouts  55 us (14%)
  blocking collectives  54.2 us (14%)
  matrix products  31.5 us (8%)
  between operations  13.6 us (3%)
  starting transfers between devices  8.38 us (2%)
    psum x1, waiting for transfers between devices, per_device(): becp = lax.psum(partial_value, ('ga', 'band'))  189 us
    all_to_all x1, blocking collectives, per_device(): lax.all_to_all(result, 'band', split_axis=0, concat_axis=2, tiled=True)  54.2 us
    all_to_all x1, waiting for transfers between devices, per_device(): lax.all_to_all(jnp.stack(jnp.split(orbitals, lax.axis_size('band'), axis=...  39.8 us
    unnamed x30, local copies, waits for them, and re-layouts  30.1 us
    dot_general x1, matrix products, project_bands(): lax.dot_general(flat_proj, stacked, (((1,), (1,)), ((), ())), preferred_e...  12.5 us
    dot_general x1, matrix products, apply_coupling(): jnp.einsum('aij,ajc->aic', matrices, blocked, precision=lax.Precision.HIG...  12.2 us
    all_to_all x1, starting transfers between devices, per_device(): lax.all_to_all(jnp.stack(jnp.split(orbitals, lax.axis_size('band'), axis=...  8.34 us
    reshape x1, local copies, waits for them, and re-layouts, apply_coupling(): blocked = becp.reshape(count, per_atom, 2 * widths)  7.92 us
  transfers between devices with their start and end apart: 2, of which 2 were waited for; matrix products, arithmetic and copies ran while one was open for 2% of the time, Pallas kernels for 0%

profile of v1, /device:TPU:0, one launch (start us, length us, event | category | flops | bytes accessed | tf_op | source)
XLA Modules:
  0.0 393.7 jit_solution(9787922111602768360)
XLA Ops:
  6.5 1.6 bitcast_dynamic-update-slice_fusion.15
  8.2 1.6 bitcast_dynamic-update-slice_fusion.14
  9.8 1.6 bitcast_dynamic-update-slice_fusion.13
  11.5 1.6 bitcast_dynamic-update-slice_fusion.12
  13.1 1.6 bitcast_dynamic-update-slice_fusion.11
  14.8 1.6 bitcast_dynamic-update-slice_fusion.10
  16.4 1.6 bitcast_dynamic-update-slice_fusion.9
  18.1 1.6 bitcast_dynamic-update-slice_fusion.8
  19.7 1.6 bitcast_dynamic-update-slice_fusion.7
  21.4 1.6 bitcast_dynamic-update-slice_fusion.6
  32.9 8.3 %all-to-all-start = ((bf16[16,64,2,512]{3,2,1,0:T(2,128)(2,1)}), bf16[16,64,2,512]{3,2,1,0:T(2,128)(2,1)S(1)}, u32[]{:S(2)}, u32[]{:S(2)}) async-start(bf16[16,64,2,512]{3,2,1,0:T(2,128)(2,1)} %bitcast_dynamic-update-slice_fusion), calls=%async_computation | async-start | bytes 4194304 | tf_op jit(solution)/shard_map/all_to_all | solution.py:63
  41.3 3.2 copy.33
  44.5 39.8 %all-to-all-done = bf16[16,64,2,512]{3,2,1,0:T(2,128)(2,1)S(1)} async-done(((bf16[16,64,2,512]{3,2,1,0:T(2,128)(2,1)}), bf16[16,64,2,512]{3,2,1,0:T(2,128)(2,1)S(1)}, u32[]{:S(2)}, u32[]{:S(2)}) %all-to-all-start) | async-done | bytes 2097184 | tf_op jit(solution)/shard_map/all_to_all | solution.py:63
  86.4 12.5 %fusion.6 = f32[864,2048]{1,0:T(8,128)} fusion(bf16[864,1024]{1,0:T(8,128)(2,1)S(1)} %bitcast.75, bf16[1024,512]{1,0:T(8,128)(2,1)S(1)} %get-tuple-element.8, bf16[1024,512]{1,0:T(8,128)(2,1)S(1)} %get-tuple-element.7, bf16[1024,1024]{1,0:T(8,128)(2,1)S(1)} %bitcast.74), kind=kOutput, calls=%fused_computation.6 | convolution fusion | flops 3636461568 | bytes 13041664 | tf_op jit(solution)/shard_map/dot_general | solution.py:39
  98.9 7.9 %reshape.35 = f32[48,18,2048]{2,1,0:T(8,128)} reshape(f32[864,2048]{1,0:T(8,128)} %fusion.6) | data formatting | bytes 14155776 | tf_op jit(solution)/shard_map/reshape | solution.py:28
  108.7 4.2 %fusion.22 = (bf16[864,1,512]{2,1,0:T(2,128)(2,1)}, bf16[864,1,512]{2,1,0:T(2,128)(2,1)}) fusion(bf16[864,2,512]{2,1,0:T(2,128)(2,1)S(1)} %copy-done), kind=kLoop, calls=%fused_computation.46 | loop fusion | bytes 3538944 | tf_op jit(solution)/shard_map/slice | solution.py:53
  112.9 189.5 %all-reduce.2.cloned.1.call-done = f32[48,18,2048]{2,1,0:T(8,128)} async-done(((f32[48,18,2048]{2,1,0:T(8,128)}), f32[48,18,2048]{2,1,0:T(8,128)}) %all-reduce.2.cloned.1.call-update) | async-done | bytes 7077904 | tf_op jit(solution)/shard_map/psum | solution.py:67
  302.4 12.2 %convolution_convert_fusion = bf16[48,18,2048]{2,1,0:T(8,128)(2,1)} fusion(f32[48,18,18]{2,1,0:T(8,128)S(1)} %copy.24, f32[48,18,2048]{2,1,0:T(8,128)} %all-reduce.2.cloned.1.call-done), kind=kOutput, calls=%fused_computation.7 | convolution fusion | flops 383975424 | bytes 10679040 | tf_op jit(solution)/shard_map/aij,ajc->aic/dot_general | solution.py:29
  314.6 4.3 %convert_element_type.12 = bf16[864,2048]{1,0:T(8,128)(2,1)S(1)} reshape(bf16[48,18,2048]{2,1,0:T(8,128)(2,1)} %convolution_convert_fusion) | data formatting | bytes 7077888 | tf_op jit(solution)/shard_map/convert_element_type | solution.py:30
  318.9 4.0 %fusion.14 = f32[2048,512]{1,0:T(8,128)S(1)} fusion(bf16[864,2048]{1,0:T(8,128)(2,1)S(1)} %convert_element_type.12, bf16[864,1,512]{2,1,0:T(2,128)(2,1)} %get-tuple-element.9), kind=kOutput, calls=%fused_computation.19 | convolution fusion | flops 1811939328 | bytes 8617984 | tf_op jit(solution)/shard_map/dot_general | solution.py:52
  323.0 2.4 fusion.15
  326.8 2.2 copy.27
  329.0 54.2 %all_to_all.23 = bf16[1024,2,512]{2,1,0:T(2,128)(2,1)S(1)} all-to-all(bf16[1024,2,512]{2,1,0:T(2,128)(2,1)S(1)} %copy.27), channel_id=1, replica_groups=mesh['ga'=2,'band'=16] {'band'}, dimensions={0} | all-to-all | bytes 4194304 | tf_op jit(solution)/shard_map/all_to_all | solution.py:70
  383.2 3.6 copy.31
  (32 shorter events, 15.2 us)
Async XLA Ops:
  32.9 51.4 %all-to-all-start = ((bf16[16,64,2,512]{3,2,1,0:T(2,128)(2,1)}), bf16[16,64,2,512]{3,2,1,0:T(2,128)(2,1)S(1)}, u32[]{:S(2)}, u32[]{:S(2)}) async-start(bf16[16,64,2,512]{3,2,1,0:T(2,128)(2,1)} %bitcast_dynamic-update-slice_fusion), calls=%async_computation | async-start | bytes 4194304 | tf_op jit(solution)/shard_map/all_to_all | solution.py:63
  41.3 261.1 %all-reduce.2.cloned.1.call-start = ((), (), s32[]{:S(2)}) async-start(), calls=%async_computation.2 | async-start | bytes 18874368 | tf_op jit(solution)/shard_map/psum | solution.py:67
  84.9 1.5 copy-start.2
  106.8 0.8 copy-start.3
  106.8 1.0 copy-start.4
  106.8 1.0 copy-start.5
  106.8 1.9 copy-start
  318.9 4.1 %copy-start.1 = (bf16[864,1,512]{2,1,0:T(2,128)(2,1)S(1)}, bf16[864,1,512]{2,1,0:T(2,128)(2,1)}, u32[]{:S(2)}) copy-start(bf16[864,1,512]{2,1,0:T(2,128)(2,1)} %get-tuple-element.10) | copy-start | bytes 2654212
Sparse Core Ops, SparseCore 0:
  107.0 195.4 all-reduce.1
